TPU v7x, 256 devices: a whole 4x4x8 slice. The times are simulated.
256 devices in a mesh: ep: 32 (over z, y), dp: 8 (over x, core).
Axes of the slice: x: 4, y: 4, z: 8, core: 2. Of those that a mesh axis runs over, the one named last changes fastest.
Arguments:
- act_in: bfloat16 [24576, 512], P(('ep', 'dp'))
- grad_out: bfloat16 [24576, 512], P(('ep', 'dp'))
- slot_ids: int32 [2, 24576, 8], P(None, ('ep', 'dp'))
- gate_vals: float32 [2, 24576, 8], P(None, ('ep', 'dp'))
- w_dense: bfloat16 [2, 512, 512], replicated
- w_gate: bfloat16 [2, 128, 512, 176], P(None, 'ep')
- w_up: bfloat16 [2, 128, 512, 176], P(None, 'ep')
- w_down: bfloat16 [2, 128, 176, 512], P(None, 'ep')
- ws_gate: bfloat16 [2, 512, 176], replicated
- ws_up: bfloat16 [2, 512, 176], replicated
- ws_down: bfloat16 [2, 176, 512], replicated
Outputs:
- output 1: bfloat16 [24576, 512], P(('ep', 'dp'))
- output 2: bfloat16 [2, 512, 512], replicated
- output 3: bfloat16 [2, 128, 512, 176], P(None, 'ep')
- output 4: bfloat16 [2, 128, 512, 176], P(None, 'ep')
- output 5: bfloat16 [2, 128, 176, 512], P(None, 'ep')
- output 6: bfloat16 [2, 512, 176], replicated
- output 7: bfloat16 [2, 512, 176], replicated
- output 8: bfloat16 [2, 176, 512], replicated
All inputs are finite; a program needn't handle non-finite values.
Results may differ from a plain program's by a relative error of at most 0.02.
Values are sent between devices in bfloat16 or wider.
A program may use at most 768 MiB of HBM per device.

v0:
```python
import jax
import jax.numpy as jnp
from jax import lax
from jax.sharding import PartitionSpec as P

ALL_AXES = ("ep", "dp")


def silu_grad(pre_act):
    sigma = jax.nn.sigmoid(pre_act)
    return sigma * (1.0 + pre_act * (1.0 - sigma))


def contract_rows(left, right):
    return lax.dot_general(left, right, (((0,), (0,)), ((), ())), preferred_element_type=jnp.float32)


def contract_cols(left, right):
    return lax.dot_general(left, right, (((1,), (1,)), ((), ())), preferred_element_type=jnp.float32)


def layer_front(act, weights, slot_ids, ep_size):
    w_dense, w_gate, w_up, w_down, ws_gate, ws_up, ws_down = weights
    tokens, width = act.shape
    top = slot_ids.shape[1]
    local_exp = w_gate.shape[0]
    capacity = 2 * tokens * top // (local_exp * ep_size)
    dense_pre = jnp.dot(act, w_dense, preferred_element_type=jnp.float32)
    mixed = (act.astype(jnp.float32) + dense_pre).astype(jnp.bfloat16)
    slot_flat = slot_ids.reshape(tokens * top)
    copy_ids = jnp.arange(1, tokens * top + 1, dtype=jnp.int32)
    slot_owner = jnp.zeros((local_exp * ep_size * capacity,), jnp.int32).at[slot_flat].set(copy_ids)
    tok_owner = (slot_owner + top - 1) // top
    mixed_ext = jnp.concatenate([jnp.zeros((1, width), mixed.dtype), mixed], axis=0)
    send_buf = jnp.take(mixed_ext, tok_owner, axis=0).reshape(ep_size, local_exp, capacity, width)
    recv_rows = lax.all_to_all(send_buf, "ep", 0, 1).reshape(local_exp, ep_size * capacity, width)
    a_one = jnp.einsum("erd,edf->erf", recv_rows, w_gate, preferred_element_type=jnp.float32)
    a_three = jnp.einsum("erd,edf->erf", recv_rows, w_up, preferred_element_type=jnp.float32)
    hidden = (jax.nn.silu(a_one) * a_three).astype(jnp.bfloat16)
    s_one = jnp.dot(mixed, ws_gate, preferred_element_type=jnp.float32)
    s_three = jnp.dot(mixed, ws_up, preferred_element_type=jnp.float32)
    shared_hidden = (jax.nn.silu(s_one) * s_three).astype(jnp.bfloat16)
    return (act, mixed, slot_flat, slot_owner, recv_rows, a_one, a_three, hidden, s_one, s_three, shared_hidden)


def layer_finish(saved, weights, gate_vals, ep_size):
    act, mixed, slot_flat, slot_owner, recv_rows, a_one, a_three, hidden, s_one, s_three, shared_hidden = saved
    w_down = weights[3]
    ws_down = weights[6]
    tokens, width = mixed.shape
    top = gate_vals.shape[1]
    local_exp = hidden.shape[0]
    capacity = recv_rows.shape[1] // ep_size
    exp_out = jnp.einsum("erf,efd->erd", hidden, w_down, preferred_element_type=jnp.float32).astype(jnp.bfloat16)
    back_rows = lax.all_to_all(exp_out.reshape(local_exp, ep_size, capacity, width), "ep", 1, 0).reshape(local_exp * ep_size * capacity, width)
    picked = jnp.take(back_rows, slot_flat, axis=0).reshape(tokens, top, width)
    routed = jnp.sum(gate_vals[:, :, None] * picked.astype(jnp.float32), axis=1)
    shared_out = jnp.dot(shared_hidden, ws_down, preferred_element_type=jnp.float32)
    return (mixed.astype(jnp.float32) + routed + shared_out).astype(jnp.bfloat16)


def layer_backward(grad_y, saved, weights, gate_vals, ep_size):
    act, mixed, slot_flat, slot_owner, recv_rows, a_one, a_three, hidden, s_one, s_three, shared_hidden = saved
    w_dense, w_gate, w_up, w_down, ws_gate, ws_up, ws_down = weights
    tokens, width = grad_y.shape
    top = gate_vals.shape[1]
    local_exp = hidden.shape[0]
    capacity = recv_rows.shape[1] // ep_size
    grad_y32 = grad_y.astype(jnp.float32)
    grad_pick = (gate_vals[:, :, None] * grad_y32[:, None, :]).astype(jnp.bfloat16).reshape(tokens * top, width)
    grad_ext = jnp.concatenate([jnp.zeros((1, width), grad_pick.dtype), grad_pick], axis=0)
    send_grad = jnp.take(grad_ext, slot_owner, axis=0).reshape(ep_size, local_exp, capacity, width)
    grad_exp_out = lax.all_to_all(send_grad, "ep", 0, 1).reshape(local_exp, ep_size * capacity, width)
    g_w_down = jnp.einsum("erf,erd->efd", hidden, grad_exp_out, preferred_element_type=jnp.float32)
    grad_hidden = jnp.einsum("erd,efd->erf", grad_exp_out, w_down, preferred_element_type=jnp.float32)
    grad_a_one = (grad_hidden * a_three * silu_grad(a_one)).astype(jnp.bfloat16)
    grad_a_three = (grad_hidden * jax.nn.silu(a_one)).astype(jnp.bfloat16)
    g_w_gate = jnp.einsum("erd,erf->edf", recv_rows, grad_a_one, preferred_element_type=jnp.float32)
    g_w_up = jnp.einsum("erd,erf->edf", recv_rows, grad_a_three, preferred_element_type=jnp.float32)
    grad_rows = (jnp.einsum("erf,edf->erd", grad_a_one, w_gate, preferred_element_type=jnp.float32) + jnp.einsum("erf,edf->erd", grad_a_three, w_up, preferred_element_type=jnp.float32)).astype(jnp.bfloat16)
    grad_back = lax.all_to_all(grad_rows.reshape(local_exp, ep_size, capacity, width), "ep", 1, 0).reshape(local_exp * ep_size * capacity, width)
    grad_routed = jnp.sum(jnp.take(grad_back, slot_flat, axis=0).reshape(tokens, top, width).astype(jnp.float32), axis=1)
    g_ws_down = contract_rows(shared_hidden, grad_y)
    grad_shared = contract_cols(grad_y, ws_down)
    grad_s_one = (grad_shared * s_three * silu_grad(s_one)).astype(jnp.bfloat16)
    grad_s_three = (grad_shared * jax.nn.silu(s_one)).astype(jnp.bfloat16)
    g_ws_gate = contract_rows(mixed, grad_s_one)
    g_ws_up = contract_rows(mixed, grad_s_three)
    grad_mixed = (grad_y32 + grad_routed + contract_cols(grad_s_one, ws_gate) + contract_cols(grad_s_three, ws_up)).astype(jnp.bfloat16)
    g_w_dense = contract_rows(act, grad_mixed)
    grad_act = (grad_mixed.astype(jnp.float32) + contract_cols(grad_mixed, w_dense)).astype(jnp.bfloat16)
    dense_grads = (g_w_dense.astype(jnp.bfloat16), g_ws_gate.astype(jnp.bfloat16), g_ws_up.astype(jnp.bfloat16), g_ws_down.astype(jnp.bfloat16))
    expert_grads = (g_w_gate.astype(jnp.bfloat16), g_w_up.astype(jnp.bfloat16), g_w_down.astype(jnp.bfloat16))
    return grad_act, dense_grads, expert_grads


def solution(mesh):
    ep_size = mesh.shape["ep"]
    tok_spec = P(ALL_AXES, None)
    route_spec = P(None, ALL_AXES, None)
    exp_spec = P(None, "ep", None, None)
    repl_spec = P(None, None, None)

    def body(act_in, grad_out, slot_ids, gate_vals, w_dense, w_gate, w_up, w_down, ws_gate, ws_up, ws_down):
        layers = w_dense.shape[0]
        all_weights = [(w_dense[layer], w_gate[layer], w_up[layer], w_down[layer], ws_gate[layer], ws_up[layer], ws_down[layer]) for layer in range(layers)]
        saved_all = []
        act = act_in
        for layer in range(layers):
            saved = layer_front(act, all_weights[layer], slot_ids[layer], ep_size)
            saved_all.append(saved)
            if layer + 1 < layers:
                act = layer_finish(saved, all_weights[layer], gate_vals[layer], ep_size)
        grad_act = grad_out
        dense_sums = [None] * layers
        expert_sums = [None] * layers
        for layer in reversed(range(layers)):
            grad_act, dense_grads, expert_grads = layer_backward(grad_act, saved_all[layer], all_weights[layer], gate_vals[layer], ep_size)
            dense_sums[layer] = [lax.psum(part, ALL_AXES) for part in dense_grads]
            expert_sums[layer] = [lax.psum(part, "dp") for part in expert_grads]
        dense_out = [jnp.stack([dense_sums[layer][which] for layer in range(layers)]) for which in range(4)]
        expert_out = [jnp.stack([expert_sums[layer][which] for layer in range(layers)]) for which in range(3)]
        return (grad_act, dense_out[0], expert_out[0], expert_out[1], expert_out[2], dense_out[1], dense_out[2], dense_out[3])

    return jax.shard_map(body, mesh=mesh, in_specs=(tok_spec, tok_spec, route_spec, route_spec, repl_spec, exp_spec, exp_spec, exp_spec, repl_spec, repl_spec, repl_spec), out_specs=(tok_spec, repl_spec, exp_spec, exp_spec, exp_spec, repl_spec, repl_spec, repl_spec), check_vma=False)
```

profile of v0, /device:TPU:1, one launch (start us, length us, event | category | flops | bytes accessed | tf_op | source)
XLA Modules:
  0.0 759.1 jit_solution(16936081201906962916)
XLA Ops:
  8.1 3.4 scatter_custom_fusion.1
  13.4 4.8 gather_fusion.1
  23.5 49.8 %all_to_all.105 = bf16[32,4,1,12,512]{4,1,3,2,0:T(4,128)(2,1)S(1)} all-to-all(bf16[32,4,1,12,512]{4,1,3,2,0:T(4,128)(2,1)S(1)} %copy.68), channel_id=1, replica_groups=mesh['ep'=32,'dp'=8] {'ep'}, dimensions={0} | all-to-all | bytes 3145728 | tf_op jit(solution)/shard_map/all_to_all | solution.py:36
  79.6 7.2 all-to-all-start.2
  87.0 3.6 scatter_custom_fusion
  91.3 5.4 gather_fusion
  97.9 28.0 %all-to-all-done.2 = bf16[1,4,32,12,512]{4,1,3,0,2:T(4,128)(2,1)} async-done(((bf16[1,4,32,12,512]{4,1,3,0,2:T(4,128)(2,1)}), bf16[1,4,32,12,512]{4,1,3,0,2:T(4,128)(2,1)}, u32[]{:S(2)}, u32[]{:S(2)}) %all-to-all-start.2) | async-done | bytes 1572896 | tf_op jit(solution)/shard_map/all_to_all | solution.py:55
  138.7 5.4 gather_fusion.3
  147.4 3.7 broadcast_in_dim_reshape.24
  151.1 4.2 copy.74
  155.4 5.9 all-to-all-start.3
  161.3 3.7 broadcast_in_dim_reshape.21
  165.0 4.2 copy.63
  169.2 29.1 %all-to-all-done.3 = bf16[32,4,1,12,512]{4,1,3,2,0:T(4,128)(2,1)S(1)} async-done(((bf16[32,4,1,12,512]{4,1,3,2,0:T(4,128)(2,1)}), bf16[32,4,1,12,512]{4,1,3,2,0:T(4,128)(2,1)S(1)}, u32[]{:S(2)}, u32[]{:S(2)}) %all-to-all-start.3) | async-done | bytes 1572896 | tf_op jit(solution)/shard_map/all_to_all | solution.py:36
  198.3 7.9 %all-to-all-start = ((bf16[32,4,1,12,512]{4,1,3,2,0:T(4,128)(2,1)}), bf16[32,4,1,12,512]{4,1,3,2,0:T(4,128)(2,1)}, u32[]{:S(2)}, u32[]{:S(2)}) async-start(bf16[32,4,1,12,512]{4,1,3,2,0:T(4,128)(2,1)} %copy.63), calls=%async_computation | async-start | bytes 3145728 | tf_op jit(solution)/shard_map/all_to_all | solution.py:73
  210.9 34.2 %all-to-all-done = bf16[32,4,1,12,512]{4,1,3,2,0:T(4,128)(2,1)} async-done(((bf16[32,4,1,12,512]{4,1,3,2,0:T(4,128)(2,1)}), bf16[32,4,1,12,512]{4,1,3,2,0:T(4,128)(2,1)}, u32[]{:S(2)}, u32[]{:S(2)}) %all-to-all-start) | async-done | bytes 1572896 | tf_op jit(solution)/shard_map/all_to_all | solution.py:73
  253.3 7.2 all-to-all-start.4
  266.1 32.2 %all-to-all-done.4 = bf16[1,4,32,12,512]{4,1,3,0,2:T(4,128)(2,1)S(1)} async-done(((bf16[1,4,32,12,512]{4,1,3,0,2:T(4,128)(2,1)}), bf16[1,4,32,12,512]{4,1,3,0,2:T(4,128)(2,1)S(1)}, u32[]{:S(2)}, u32[]{:S(2)}) %all-to-all-start.4) | async-done | bytes 1572896 | tf_op jit(solution)/shard_map/all_to_all | solution.py:81
  309.9 5.4 gather_fusion.5
  321.7 45.1 %all_to_all.106 = bf16[32,4,1,12,512]{4,1,3,2,0:T(4,128)(2,1)S(1)} all-to-all(bf16[32,4,1,12,512]{4,1,3,2,0:T(4,128)(2,1)S(1)} %copy.81), channel_id=1, replica_groups=mesh['ep'=32,'dp'=8] {'ep'}, dimensions={0} | all-to-all | bytes 3145728 | tf_op jit(solution)/shard_map/all_to_all | solution.py:73
  373.1 6.3 all-to-all-start.6
  399.1 17.1 %all-to-all-done.6 = bf16[1,4,32,12,512]{4,1,3,0,2:T(4,128)(2,1)} async-done(((bf16[1,4,32,12,512]{4,1,3,0,2:T(4,128)(2,1)}), bf16[1,4,32,12,512]{4,1,3,0,2:T(4,128)(2,1)}, u32[]{:S(2)}, u32[]{:S(2)}) %all-to-all-start.6) | async-done | bytes 1572896 | tf_op jit(solution)/shard_map/all_to_all | solution.py:81
  427.0 41.5 %all-reduce.11.cloned.1.call-done = (bf16[1,4,512,176]{2,3,1,0:T(8,128)(2,1)}, bf16[1,4,512,176]{2,3,1,0:T(8,128)(2,1)}, bf16[1,4,512,176]{2,3,1,0:T(8,128)(2,1)...) async-done(((bf16[1,4,512,176]{2,3,1,0:T(8,128)(2,1)}, bf16[1,4,512,176]{2,3,1,0:T(8,128)(2,1)}, ...) | async-done | bytes 4325392 | tf_op jit(solution)/shard_map/psum | solution.py:120
  475.2 271.5 %all-reduce.9.cloned.1.call-done = (bf16[1,512,512]{1,2,0:T(8,128)(2,1)}, bf16[1,512,512]{1,2,0:T(8,128)(2,1)}, bf16[1,512,176]{1,2,0:T(8,128)(2,1)}, bf16[1,512...) async-done(((bf16[1,512,512]{1,2,0:T(8,128)(2,1)}, ...) | async-done | bytes 2129936 | tf_op jit(solution)/shard_map/psum | solution.py:119
  (253 shorter events, 116.7 us)
Async XLA Ops:
  23.5 49.8 %copy-start.16 = (bf16[2,4,512,176]{2,3,1,0:T(8,128)(2,1)S(1)}, bf16[2,4,512,176]{2,3,1,0:T(8,128)(2,1)}, u32[]{:S(2)}) copy-start(bf16[2,4,512,176]{2,3,1,0:T(8,128)(2,1)} %param.22) | copy-start | bytes 4325380
  79.6 11.0 %copy-start.63 = (f32[2,96,8]{1,2,0:T(8,128)S(1)}, f32[2,96,8]{1,2,0:T(8,128)}, u32[]{:S(2)}) copy-start(f32[2,96,8]{1,2,0:T(8,128)} %param.20) | copy-start | bytes 18436
  79.6 11.3 %copy-start.32 = (bf16[96,512]{1,0:T(8,128)(2,1)S(1)}, bf16[96,512]{1,0:T(8,128)(2,1)}, u32[]{:S(2)}) copy-start(bf16[96,512]{1,0:T(8,128)(2,1)} %param.18) | copy-start | bytes 294916
  79.6 46.4 %all-to-all-start.2 = ((bf16[1,4,32,12,512]{4,1,3,0,2:T(4,128)(2,1)}), bf16[1,4,32,12,512]{4,1,3,0,2:T(4,128)(2,1)}, u32[]{:S(2)}, u32[]{:S(2)}) async-start(bf16[1,4,32,12,512]{4,1,3,0,2:T(4,128)(2,1)} %bitcast.16), calls=%async_computation.2 | async-start | bytes 3145728 | tf_op jit(solution)/shard_map/all_to_all | solution.py:55
  91.3 5.5 copy-start.14
  91.3 5.7 copy-start.23
  96.9 38.2 %copy-start.61 = (pred[768]{0:T(1024)(128)(4,1)}, pred[768]{0:T(1024)(128)(4,1)S(1)}, u32[]{:S(2)}) copy-start(pred[768]{0:T(1024)(128)(4,1)S(1)} %compare_and_fusion.5) | copy-start | bytes 2308
  97.1 32.2 %copy-start.54 = (f32[96,176]{0,1:T(8,128)}, f32[96,176]{0,1:T(8,128)S(1)}, u32[]{:S(2)}) copy-start(f32[96,176]{0,1:T(8,128)S(1)} %fusion.104) | copy-start | bytes 202756
  97.9 38.9 %copy-start.40 = (bf16[96,176]{0,1:T(8,128)(2,1)}, bf16[96,176]{0,1:T(8,128)(2,1)S(1)}, u32[]{:S(2)}) copy-start(bf16[96,176]{0,1:T(8,128)(2,1)S(1)} %get-tuple-element.68) | copy-start | bytes 101380
  138.7 5.5 copy-start.2
  155.4 43.0 %all-to-all-start.3 = ((bf16[32,4,1,12,512]{4,1,3,2,0:T(4,128)(2,1)}), bf16[32,4,1,12,512]{4,1,3,2,0:T(4,128)(2,1)S(1)}, u32[]{:S(2)}, u32[]{:S(2)}) async-start(bf16[32,4,1,12,512]{4,1,3,2,0:T(4,128)(2,1)} %copy.74), calls=%async_computation.3 | async-start | bytes 3145728 | tf_op jit(solution)/shard_map/all_to_all | solution.py:36
  198.3 10.8 %copy-start = (bf16[32,4,1,12,512]{4,1,3,2,0:T(4,128)(2,1)}, bf16[32,4,1,12,512]{4,1,3,2,0:T(4,128)(2,1)S(1)}, u32[]{:S(2)}) copy-start(bf16[32,4,1,12,512]{4,1,3,2,0:T(4,128)(2,1)S(1)} %all-to-all-done.3) | copy-start | bytes 4718596
  198.3 46.8 %all-to-all-start = ((bf16[32,4,1,12,512]{4,1,3,2,0:T(4,128)(2,1)}), bf16[32,4,1,12,512]{4,1,3,2,0:T(4,128)(2,1)}, u32[]{:S(2)}, u32[]{:S(2)}) async-start(bf16[32,4,1,12,512]{4,1,3,2,0:T(4,128)(2,1)} %copy.63), calls=%async_computation | async-start | bytes 3145728 | tf_op jit(solution)/shard_map/all_to_all | solution.py:73
  253.3 11.1 %copy-start.33 = (bf16[96,512]{1,0:T(8,128)(2,1)S(1)}, bf16[96,512]{1,0:T(8,128)(2,1)}, u32[]{:S(2)}) copy-start(bf16[96,512]{1,0:T(8,128)(2,1)} %param.18) | copy-start | bytes 294916
  253.3 45.0 %all-to-all-start.4 = ((bf16[1,4,32,12,512]{4,1,3,0,2:T(4,128)(2,1)}), bf16[1,4,32,12,512]{4,1,3,0,2:T(4,128)(2,1)S(1)}, u32[]{:S(2)}, u32[]{:S(2)}) async-start(bf16[1,4,32,12,512]{4,1,3,0,2:T(4,128)(2,1)} %bitcast.225), calls=%async_computation.4 | async-start | bytes 3145728 | tf_op jit(solution)/shard_map/all_to_all | solution.py:81
  266.1 41.7 %copy-start.42 = (bf16[96,176]{0,1:T(8,128)(2,1)}, bf16[96,176]{0,1:T(8,128)(2,1)S(1)}, u32[]{:S(2)}) copy-start(bf16[96,176]{0,1:T(8,128)(2,1)S(1)} %get-tuple-element.60) | copy-start | bytes 101380
  318.5 48.2 %copy-start.70 = (f32[4,384,176]{1,2,0:T(8,128)S(1)}, f32[4,384,176]{1,2,0:T(8,128)}, u32[]{:S(2)}) copy-start(f32[4,384,176]{1,2,0:T(8,128)} %get-tuple-element.71) | copy-start | bytes 3244036
  321.6 45.1 %copy-start.36 = (bf16[2,4,176,512]{3,2,1,0:T(8,128)(2,1)S(1)}, bf16[2,4,176,512]{3,2,1,0:T(8,128)(2,1)}, u32[]{:S(2)}) copy-start(bf16[2,4,176,512]{3,2,1,0:T(8,128)(2,1)} %param.24) | copy-start | bytes 4325380
  321.7 45.1 %copy-start.66 = (f32[4,384,176]{1,2,0:T(8,128)S(1)}, f32[4,384,176]{1,2,0:T(8,128)}, u32[]{:S(2)}) copy-start(f32[4,384,176]{1,2,0:T(8,128)} %copy-done.65) | copy-start | bytes 3244036
  373.1 6.4 copy-start.1
  373.1 43.1 %all-to-all-start.6 = ((bf16[1,4,32,12,512]{4,1,3,0,2:T(4,128)(2,1)}), bf16[1,4,32,12,512]{4,1,3,0,2:T(4,128)(2,1)}, u32[]{:S(2)}, u32[]{:S(2)}) async-start(bf16[1,4,32,12,512]{4,1,3,0,2:T(4,128)(2,1)} %bitcast.223), calls=%async_computation.6 | async-start | bytes 3145728 | tf_op jit(solution)/shard_map/all_to_all | solution.py:81
  379.4 89.1 %all-reduce.11.cloned.1.call-start = ((), (), s32[]{:S(2)}) async-start(), calls=%async_computation.8 | async-start | bytes 8650752 | tf_op jit(solution)/shard_map/psum | solution.py:120
  391.9 6.1 copy-start.31
  391.9 354.9 %all-reduce.9.cloned.1.call-start = ((), (), s32[]{:S(2)}) async-start(), calls=%async_computation.7 | async-start | bytes 4259840 | tf_op jit(solution)/shard_map/psum | solution.py:119
  (54 other events, 118.5 us)
Sparse Core Ops, SparseCore 0:
  392.0 76.4 all-reduce.10
  475.5 271.1 all-reduce.8
where the time goes:
time: 769 us; the launch traced here: 759 us
  waiting for transfers between devices  454 us (59%)
  blocking collectives  94.9 us (12%)
  local copies, waits for them, and re-layouts  93.9 us (12%)
  matrix products  45.4 us (6%)
  starting transfers between devices  34.9 us (5%)
  other arithmetic  20.9 us (3%)
  between operations  15.4 us (2%)
    psum x1, waiting for transfers between devices, body(): dense_sums[layer] = [lax.psum(part, ALL_AXES) for part in dense_grads]  272 us
    all_to_all x1, blocking collectives, layer_front(): lax.all_to_all(send_buf, 'ep', 0, 1)  49.8 us
    all_to_all x2, waiting for transfers between devices, layer_backward(): lax.all_to_all(grad_rows.reshape(local_exp, ep_size, capacity, width), 'e...  49.3 us
    all_to_all x1, blocking collectives, layer_backward(): lax.all_to_all(send_grad, 'ep', 0, 1)  45.1 us
    psum x1, waiting for transfers between devices, body(): expert_sums[layer] = [lax.psum(part, 'dp') for part in expert_grads]  41.5 us
    all_to_all x1, waiting for transfers between devices, layer_backward(): lax.all_to_all(send_grad, 'ep', 0, 1)  34.2 us
    all_to_all x1, waiting for transfers between devices, layer_front(): lax.all_to_all(send_buf, 'ep', 0, 1)  29.1 us
    all_to_all x1, waiting for transfers between devices, layer_finish(): lax.all_to_all(exp_out.reshape(local_exp, ep_size, capacity, width), 'ep'...  28 us
  transfers between devices with their start and end apart: 7, of which 7 were waited for; matrix products, arithmetic and copies ran while one was open for 8% of the time, Pallas kernels for 0%

commit v1 on v0

v1 whole, which is shorter than its diff:
```python
import functools
import jax
import jax.numpy as jnp
from jax import lax
from jax.experimental import pallas as pl
from jax.experimental.pallas import tpu as pltpu
from jax.sharding import PartitionSpec as P

ALL_AXES = ("ep", "dp")
MESH = pl.DeviceIdType.MESH
F32 = jnp.float32
BF16 = jnp.bfloat16
NY = 4
LOCAL_EXP = 4
INFO_ROWS = 16
FIRST_ROWS = 64
LANES = 128


def nn(a, b):
    return lax.dot_general(a, b, (((1,), (0,)), ((), ())), preferred_element_type=F32)


def nt(a, b):
    return lax.dot_general(a, b, (((1,), (1,)), ((), ())), preferred_element_type=F32)


def tn(a, b):
    return lax.dot_general(a, b, (((0,), (0,)), ((), ())), preferred_element_type=F32)


def sigmoid(a):
    return 1.0 / (1.0 + jnp.exp(-a))


def split3(value):
    high = value.astype(BF16)
    rest = value - high.astype(F32)
    mid = rest.astype(BF16)
    low = (rest - mid.astype(F32)).astype(BF16)
    return high, mid, low


def ring_span(size, even):
    plus, minus = size // 2, (size - 1) // 2
    return range(-minus, plus + 1) if even else range(-plus, minus + 1)


def sign(v):
    return (v > 0) - (v < 0)


def gather_plan(nz, ny):
    nodes = []
    for kz in ring_span(nz, True):
        for ky in ring_span(ny, kz % 2 == 0):
            nodes.append((0, kz, ky))
    for ky in ring_span(ny, True):
        for kz in ring_span(nz, ky % 2 == 0):
            nodes.append((1, kz, ky))
    nodes = [n for n in nodes if n[1] or n[2]]
    nodes.sort(key=lambda n: abs(n[1]) + abs(n[2]))
    return nodes


def parent_of(node):
    part, kz, ky = node
    if part == 0:
        return (part, kz, ky - sign(ky)) if ky else (part, kz - sign(kz), 0)
    return (part, kz - sign(kz), ky) if kz else (part, 0, ky - sign(ky))


class Gather:
    def __init__(self, buf, splits, send, recv, me, nz, dp):
        self.buf, self.splits, self.send, self.recv = buf, splits, send, recv
        self.nz, self.dp = nz, dp
        self.z, self.y = me // NY, me % NY
        self.nodes = gather_plan(nz, NY)
        self.ids = {node: i for i, node in enumerate(self.nodes)}
        self.children = {}
        for node in self.nodes:
            self.children.setdefault(parent_of(node), []).append(node)

    def ep_at(self, dz, dy):
        return ((self.z + dz + 2 * self.nz) % self.nz) * NY + (self.y + dy + 2 * NY) % NY

    def block(self, part, kz, ky):
        low, high = self.splits[part], self.splits[part + 1]
        return self.buf.at[self.ep_at(-kz, -ky), pl.ds(low, high - low)]

    def out_copy(self, node):
        part, pz, py = parent_of(node)
        ref = self.block(part, pz, py)
        i = self.ids[node]
        target = self.ep_at(node[1] - pz, node[2] - py)
        return pltpu.make_async_remote_copy(src_ref=ref, dst_ref=ref, send_sem=self.send.at[i], recv_sem=self.recv.at[i], device_id=(target, self.dp), device_id_type=MESH)

    def in_copy(self, node):
        part, pz, py = parent_of(node)
        ref = self.block(*node)
        i = self.ids[node]
        source = self.ep_at(pz - node[1], py - node[2])
        return pltpu.make_async_remote_copy(src_ref=ref, dst_ref=ref, send_sem=self.send.at[i], recv_sem=self.recv.at[i], device_id=(source, self.dp), device_id_type=MESH)

    def begin(self):
        for part in (0, 1):
            for child in self.children[(part, 0, 0)]:
                self.out_copy(child).start()

    def rounds(self):
        by_hops = {}
        for node in self.nodes:
            by_hops.setdefault(abs(node[1]) + abs(node[2]), []).append(node)
        return [by_hops[h] for h in sorted(by_hops)]

    def advance(self, nodes):
        for node in nodes:
            self.in_copy(node).wait_recv()
            for child in self.children.get(node, ()):
                self.out_copy(child).start()

    def finish(self):
        for node in self.nodes:
            self.out_copy(node).wait_send()


class Exchange:
    def __init__(self, src, dst, send, recv, me, nz, dp):
        self.src, self.dst, self.send, self.recv, self.nz, self.dp, self.me = src, dst, send, recv, nz, dp, me
        self.z, self.y = me // NY, me % NY

    def ep_at(self, dz, dy):
        return ((self.z + dz + self.nz) % self.nz) * NY + (self.y + dy + NY) % NY

    def order(self):
        half = []
        for k in range(1, self.nz // 2 + 1):
            half += [k] if 2 * k == self.nz else [k, self.nz - k]
        return half + [0]

    def copy(self, dz, dy, peer, block, slot):
        i = dz * NY + dy
        return pltpu.make_async_remote_copy(src_ref=self.src.at[block], dst_ref=self.dst.at[slot], send_sem=self.send.at[i], recv_sem=self.recv.at[i], device_id=(peer, self.dp), device_id_type=MESH)

    def start(self, dz):
        for dy in range(NY):
            if dz or dy:
                peer = self.ep_at(dz, dy)
                self.copy(dz, dy, peer, peer, self.me).start()
        if dz == 0:
            self.dst[self.me] = self.src[self.me]

    def wait_all(self):
        for dz in self.order():
            for dy in range(NY):
                if dz or dy:
                    peer = self.ep_at(-dz, -dy)
                    self.copy(dz, dy, peer, peer, peer).wait_recv()

    def finish(self):
        for dz in range(self.nz):
            for dy in range(NY):
                if dz or dy:
                    peer = self.ep_at(dz, dy)
                    self.copy(dz, dy, peer, peer, self.me).wait_send()


def enter(me, ep, dp):
    barrier = pltpu.get_barrier_semaphore()

    def hello(off, carry):
        pl.semaphore_signal(barrier, inc=1, device_id=((me + off) % ep, dp), device_id_type=MESH)
        return carry

    lax.fori_loop(1, ep, hello, 0)
    pl.semaphore_wait(barrier, ep - 1)


def info_block(slots, gates):
    top, tokens = slots.shape
    high_slot = slots // 16
    low_slot = slots - high_slot * 16
    high, mid, low = split3(gates)
    pad = jnp.zeros((top, LANES - tokens), BF16)

    def wide(rows):
        return jnp.concatenate([rows, pad], axis=1)

    upper = jnp.concatenate([wide(high_slot.astype(F32).astype(BF16)), wide(low_slot.astype(F32).astype(BF16)), wide(high), wide(mid)], axis=1)
    lower = jnp.concatenate([wide(low), jnp.zeros((top, 3 * LANES), BF16)], axis=1)
    return upper, lower


def build_select(s_group, info_ref, tgt_ref, first_slot, select_ref, gate_ref, top, per_exp):
    rows = LOCAL_EXP * NY * per_exp
    row_gate = jnp.zeros((rows, 1), F32)
    for si in range(NY):
        src = s_group * NY + si
        info = info_ref[src].astype(F32)
        slot = info[0:top, 0:LANES] * 16.0 + info[0:top, LANES:2 * LANES]
        gate = info[0:top, 2 * LANES:3 * LANES] + info[0:top, 3 * LANES:4 * LANES] + info[8:8 + top, 0:LANES]
        slot = slot - first_slot
        lane = lax.broadcasted_iota(jnp.int32, slot.shape, 1)
        slot = jnp.where(lane < 96, slot, -2000000.0)
        target = tgt_ref[si]
        found = jnp.full((rows, LANES), -1.0, F32)
        for j in range(top):
            found = jnp.where(slot[j:j + 1, :] == target, gate[j:j + 1, :], found)
        select_ref[src] = jnp.where(found >= 0.0, 1.0, 0.0).astype(BF16)
        row_gate = row_gate + jnp.sum(jnp.maximum(found, 0.0), axis=1, keepdims=True)
    gate_ref[s_group] = jnp.broadcast_to(row_gate, (rows, LANES))


def init_targets(tgt_ref, perm_ref, per_exp):
    rows = LOCAL_EXP * NY * per_exp
    row = lax.broadcasted_iota(jnp.int32, (rows, LANES), 0)
    expert = row // (NY * per_exp)
    rest = row - expert * (NY * per_exp)
    source = rest // per_exp
    slot = expert * per_exp + rest - source * per_exp
    for si in range(NY):
        tgt_ref[si] = jnp.where(source == si, slot, -1000000).astype(F32)
    out_row = lax.broadcasted_iota(jnp.int32, (rows, rows), 0)
    in_row = lax.broadcasted_iota(jnp.int32, (rows, rows), 1)
    out_source = out_row // (LOCAL_EXP * per_exp)
    out_rest = out_row - out_source * (LOCAL_EXP * per_exp)
    out_expert = out_rest // per_exp
    wanted = out_expert * (NY * per_exp) + out_source * per_exp + out_rest - out_expert * per_exp
    perm_ref[...] = jnp.where(in_row == wanted, 1.0, 0.0).astype(BF16)


def expand(s_group, select_ref, block_ref, tokens):
    total = None
    for si in range(NY):
        src = s_group * NY + si
        part = nn(select_ref[src][:, :tokens], block_ref[src, 0:tokens])
        total = part if total is None else total + part
    return total


def scatter_rows(s_group, rows32, dst_ref, per_exp):
    size = NY * per_exp
    values = rows32.astype(BF16)
    for e in range(LOCAL_EXP):
        dst_ref[e, pl.ds(pl.multiple_of(s_group * size, 16), size)] = values[e * size:(e + 1) * size]


def permute_group(s_group, src_ref, perm_ref, out_ref, per_exp):
    size = NY * per_exp
    rows = jnp.concatenate([src_ref[e, pl.ds(pl.multiple_of(s_group * size, 16), size)] for e in range(LOCAL_EXP)], axis=0)
    mixed = nn(perm_ref[...], rows).astype(BF16)
    for si in range(NY):
        out_ref[s_group * NY + si] = mixed[si * LOCAL_EXP * per_exp:(si + 1) * LOCAL_EXP * per_exp]


def slot_matrix(slot_cols, gate_cols, dst_ref, tokens, top, n_slots):
    step = 3 * LANES
    for c in range(n_slots // step):
        lane = (lax.broadcasted_iota(jnp.int32, (tokens, step), 1) + c * step).astype(F32)
        found = jnp.zeros((tokens, step), F32)
        for j in range(top):
            value = 1.0 if gate_cols is None else gate_cols[:, j:j + 1]
            found = jnp.where(slot_cols[:, j:j + 1] == lane, value, found)
        cols = pl.ds(c * step, step)
        if gate_cols is None:
            dst_ref[:, cols] = found.astype(BF16)
        else:
            for k, piece in enumerate(split3(found)):
                dst_ref[k * tokens:(k + 1) * tokens, cols] = piece


def forward_kernel(dims, x_ref, dy_ref, slots_ref, gates_ref, slot_cols_ref, gate_cols_ref, wd_ref, w1_hbm, w3_hbm, w2_hbm, ws1_ref, ws3_ref, ws2_ref,
                   u_out, rows_out, select_out, gate_out, dy_all, x2_out,
                   u_all, w1, w3, w2, tgt, perm, exp_out, send_buf, recv_buf, slot_mat, gsend, grecv, dsend, drecv, asend, arecv, wsem):
    ep, tokens, top, per_exp = dims
    nz = ep // NY
    me, dp = lax.axis_index("ep"), lax.axis_index("dp")
    loads = [pltpu.make_async_copy(h, v, wsem.at[i]) for i, (h, v) in enumerate([(w1_hbm, w1), (w3_hbm, w3), (w2_hbm, w2)])]
    for load in loads:
        load.start()
    x = x_ref[...]
    u32 = x.astype(F32) + nn(x, wd_ref[...])
    u = u32.astype(BF16)
    u_all[me, 0:tokens] = u
    upper, lower = info_block(slots_ref[0], gates_ref[0])
    u_all[me, tokens:tokens + top] = upper
    u_all[me, tokens + 8:tokens + 8 + top] = lower
    u_out[...] = u
    dy_all[me, 0:tokens] = dy_ref[...]
    upper, lower = info_block(slots_ref[1], gates_ref[1])
    dy_all[me, tokens:tokens + top] = upper
    dy_all[me, tokens + 8:tokens + 8 + top] = lower
    enter(me, ep, dp)
    splits = (0, FIRST_ROWS, tokens + INFO_ROWS)
    gather = Gather(u_all, splits, gsend, grecv, me, nz, dp)
    gather.begin()
    init_targets(tgt, perm, per_exp)
    slot_matrix(slot_cols_ref[...], gate_cols_ref[...], slot_mat, tokens, top, ep * LOCAL_EXP * per_exp)
    for nodes in gather.rounds():
        gather.advance(nodes)
    late = Gather(dy_all, splits, dsend, drecv, me, nz, dp)
    late.begin()
    first_slot = (me * (LOCAL_EXP * per_exp)).astype(F32)

    def fill(g, carry):
        build_select(g, u_all.at[:, pl.ds(tokens, INFO_ROWS)], tgt, first_slot, select_out, gate_out, top, per_exp)
        scatter_rows(g, expand(g, select_out, u_all, tokens), rows_out, per_exp)
        return carry

    lax.fori_loop(0, nz, fill, 0)
    for load in loads:
        load.wait()

    def experts(e, carry):
        rows = rows_out[e]
        a_one = nt(rows, w1[e])
        a_three = nt(rows, w3[e])
        hidden = (a_one * sigmoid(a_one) * a_three).astype(BF16)
        exp_out[e] = nn(hidden, w2[e]).astype(BF16)
        return carry

    lax.fori_loop(0, LOCAL_EXP, experts, 0)
    back = Exchange(send_buf, recv_buf, asend, arecv, me, nz, dp)
    for dz in back.order():
        permute_group((back.z + dz) % nz, exp_out, perm, send_buf, per_exp)
        back.start(dz)
    s_one = nt(u, ws1_ref[...])
    s_three = nt(u, ws3_ref[...])
    shared_hidden = (s_one * sigmoid(s_one) * s_three).astype(BF16)
    base = u.astype(F32) + nn(shared_hidden, ws2_ref[...])
    for nodes in late.rounds():
        late.advance(nodes)
    back.wait_all()
    picked = nn(slot_mat[...], recv_buf[...].reshape(ep * LOCAL_EXP * per_exp, recv_buf.shape[2]))
    routed = picked[0:tokens] + picked[tokens:2 * tokens] + picked[2 * tokens:3 * tokens]
    x2_out[...] = (base + routed).astype(BF16)
    gather.finish()
    late.finish()
    back.finish()


def backward_kernel(dims, second, *refs):
    ep, tokens, top, per_exp = dims
    nz = ep // NY
    if second:
        (x_ref, dy_ref, slot_cols_ref, wd_ref, w1_hbm, w3_hbm, w2_hbm, ws1_ref, ws3_ref, ws2_ref, dy_all,
         dx_out, g_wd, g_w1, g_w3, g_w2, g_ws1, g_ws3, g_ws2,
         rows, gate, select, block_all, w1, w3, w2, tgt, perm, grad_rows, exp_out, send_buf, recv_buf, slot_mat, gsend, grecv, asend, arecv, wsem) = refs
    else:
        (x_ref, dy_ref, slot_cols_ref, wd_ref, w1_hbm, w3_hbm, w2_hbm, ws1_ref, ws3_ref, ws2_ref, u_ref, rows, gate, select,
         dx_out, g_wd, g_w1, g_w3, g_w2, g_ws1, g_ws3, g_ws2,
         block_all, w1, w3, w2, tgt, perm, grad_rows, exp_out, send_buf, recv_buf, slot_mat, gsend, grecv, asend, arecv, wsem) = refs
    me, dp = lax.axis_index("ep"), lax.axis_index("dp")
    loads = [pltpu.make_async_copy(h, v, wsem.at[i]) for i, (h, v) in enumerate([(w1_hbm, w1), (w3_hbm, w3), (w2_hbm, w2)])]
    for load in loads:
        load.start()
    x = x_ref[...]
    dy = dy_ref[...]
    if second:
        u = (x.astype(F32) + nn(x, wd_ref[...])).astype(BF16)
        block_all[me] = u
    else:
        u = u_ref[...]
        block_all[me] = dy
    enter(me, ep, dp)
    gather = Gather(block_all, (0, FIRST_ROWS, tokens), gsend, grecv, me, nz, dp)
    gather.begin()
    init_targets(tgt, perm, per_exp)
    slot_matrix(slot_cols_ref[...], None, slot_mat, tokens, top, ep * LOCAL_EXP * per_exp)
    first_slot = (me * (LOCAL_EXP * per_exp)).astype(F32)

    def gated(g, source_ref):
        rows32 = expand(g, select, source_ref, tokens)
        scale = jnp.concatenate([gate[g]] * (rows32.shape[1] // LANES), axis=1)
        scatter_rows(g, rows32 * scale, grad_rows, per_exp)

    def early(g, carry):
        build_select(g, dy_all.at[:, pl.ds(tokens, INFO_ROWS)], tgt, first_slot, select, gate, top, per_exp)
        gated(g, dy_all)
        return carry

    rounds = gather.rounds()
    share = -(-nz // len(rounds))
    for i, nodes in enumerate(rounds):
        gather.advance(nodes)
        if second:
            low, high = min(i * share, nz), min((i + 1) * share, nz)
            if high > low:
                lax.fori_loop(low, high, early, 0)

    def fill(g, carry):
        if second:
            scatter_rows(g, expand(g, select, block_all, tokens), rows, per_exp)
        else:
            gated(g, block_all)
        return carry

    lax.fori_loop(0, nz, fill, 0)
    for load in loads:
        load.wait()

    def experts(e, carry):
        x_rows = rows[e]
        g_rows = grad_rows[e]
        a_one = nt(x_rows, w1[e])
        a_three = nt(x_rows, w3[e])
        sig = sigmoid(a_one)
        silu = a_one * sig
        hidden = (silu * a_three).astype(BF16)
        g_hidden = nt(g_rows, w2[e])
        g_one = (g_hidden * a_three * (sig * (1.0 + a_one * (1.0 - sig)))).astype(BF16)
        g_three = (g_hidden * silu).astype(BF16)
        exp_out[e] = (nn(g_one, w1[e]) + nn(g_three, w3[e])).astype(BF16)
        g_w1[e] = tn(g_one, x_rows).astype(BF16)
        g_w3[e] = tn(g_three, x_rows).astype(BF16)
        g_w2[e] = tn(hidden, g_rows).astype(BF16)
        return carry

    lax.fori_loop(0, LOCAL_EXP, experts, 0)
    back = Exchange(send_buf, recv_buf, asend, arecv, me, nz, dp)
    for dz in back.order():
        permute_group((back.z + dz) % nz, exp_out, perm, send_buf, per_exp)
        back.start(dz)
    s_one = nt(u, ws1_ref[...])
    s_three = nt(u, ws3_ref[...])
    sig = sigmoid(s_one)
    silu = s_one * sig
    shared_hidden = (silu * s_three).astype(BF16)
    g_ws2[...] = tn(shared_hidden, dy).astype(BF16)
    g_shared = nt(dy, ws2_ref[...])
    g_one = (g_shared * s_three * (sig * (1.0 + s_one * (1.0 - sig)))).astype(BF16)
    g_three = (g_shared * silu).astype(BF16)
    g_ws1[...] = tn(g_one, u).astype(BF16)
    g_ws3[...] = tn(g_three, u).astype(BF16)
    base = dy.astype(F32) + nn(g_one, ws1_ref[...]) + nn(g_three, ws3_ref[...])
    back.wait_all()
    routed = nn(slot_mat[...], recv_buf[...].reshape(ep * LOCAL_EXP * per_exp, recv_buf.shape[2]))
    g_mixed = (base + routed).astype(BF16)
    dx_out[...] = (g_mixed.astype(F32) + nt(g_mixed, wd_ref[...])).astype(BF16)
    g_wd[...] = tn(x, g_mixed).astype(BF16)
    gather.finish()
    back.finish()


def vmem():
    return pl.BlockSpec(memory_space=pltpu.VMEM)


def hbm():
    return pl.BlockSpec(memory_space=pl.ANY)


def params(cid):
    return pltpu.CompilerParams(collective_id=cid, has_side_effects=True, vmem_limit_bytes=60 * 1024 * 1024)


def comm_sems(ep, gathers):
    hops = 2 * (ep - 1)
    dma = pltpu.SemaphoreType.DMA
    return [dma((hops,)) for _ in range(2 * gathers)] + [dma((ep,)), dma((ep,)), dma((3,))]


def forward_layer(ep, x, dy, slots, gates, slot_cols, gate_cols, weights):
    wd, w1, w3, w2, ws1, ws3, ws2 = weights
    tokens, width = x.shape
    top = slots.shape[1]
    hid = w1.shape[1]
    per_exp = 2 * tokens * top // (LOCAL_EXP * ep)
    nz = ep // NY
    group = LOCAL_EXP * NY * per_exp
    sds = jax.ShapeDtypeStruct
    outs = [
        sds((tokens, width), BF16),
        sds((LOCAL_EXP, ep * per_exp, width), BF16),
        sds((ep, group, LANES), BF16),
        sds((nz, group, LANES), F32),
        sds((ep, tokens + INFO_ROWS, width), BF16),
        sds((tokens, width), BF16),
    ]
    v = pltpu.VMEM
    scratch = [
        v((ep, tokens + INFO_ROWS, width), BF16),
        v((LOCAL_EXP, hid, width), BF16), v((LOCAL_EXP, hid, width), BF16), v((LOCAL_EXP, hid, width), BF16),
        v((NY, group, LANES), F32), v((group, group), BF16),
        v((LOCAL_EXP, ep * per_exp, width), BF16),
        v((ep, LOCAL_EXP * per_exp, width), BF16), v((ep, LOCAL_EXP * per_exp, width), BF16),
        v((3 * tokens, ep * LOCAL_EXP * per_exp), BF16),
    ] + comm_sems(ep, 2)
    return pl.pallas_call(
        functools.partial(forward_kernel, (ep, tokens, top, per_exp)),
        out_shape=outs,
        in_specs=[vmem()] * 7 + [hbm()] * 3 + [vmem()] * 3,
        out_specs=[vmem()] * 6,
        scratch_shapes=scratch,
        compiler_params=params(0),
        name="forward_layer",
    )(x, dy, slots, gates, slot_cols, gate_cols, wd, w1, w3, w2, ws1, ws3, ws2)


def backward_layer(ep, cid, second, x, dy, slot_cols, weights, extra):
    wd, w1, w3, w2, ws1, ws3, ws2 = weights
    tokens, width = x.shape
    top = slot_cols.shape[1]
    hid = w1.shape[1]
    shid = ws1.shape[0]
    per_exp = 2 * tokens * top // (LOCAL_EXP * ep)
    nz = ep // NY
    group = LOCAL_EXP * NY * per_exp
    sds = jax.ShapeDtypeStruct
    outs = [sds((tokens, width), BF16), sds((width, width), BF16)] + [sds((LOCAL_EXP, hid, width), BF16)] * 3 + [sds((shid, width), BF16)] * 3
    v = pltpu.VMEM
    row_buf = v((LOCAL_EXP, ep * per_exp, width), BF16)
    scratch = [row_buf, v((nz, group, LANES), F32), v((ep, group, LANES), BF16)] if second else []
    scratch += [
        v((ep, tokens, width), BF16),
        v((LOCAL_EXP, hid, width), BF16), v((LOCAL_EXP, hid, width), BF16), v((LOCAL_EXP, hid, width), BF16),
        v((NY, group, LANES), F32), v((group, group), BF16),
        row_buf, row_buf,
        v((ep, LOCAL_EXP * per_exp, width), BF16), v((ep, LOCAL_EXP * per_exp, width), BF16),
        v((tokens, ep * LOCAL_EXP * per_exp), BF16),
    ] + comm_sems(ep, 1)
    return pl.pallas_call(
        functools.partial(backward_kernel, (ep, tokens, top, per_exp), second),
        out_shape=outs,
        in_specs=[vmem()] * 4 + [hbm()] * 3 + [vmem()] * (3 + len(extra)),
        out_specs=[vmem()] * 8,
        scratch_shapes=scratch,
        compiler_params=params(cid),
        name="backward_second" if second else "backward_first",
    )(x, dy, slot_cols, wd, w1, w3, w2, ws1, ws3, ws2, *extra)


def solution(mesh):
    ep = mesh.shape["ep"]
    tok_spec = P(ALL_AXES, None)
    route_spec = P(None, ALL_AXES, None)
    exp_spec = P(None, "ep", None, None)
    repl_spec = P(None, None, None)

    def body(act_in, grad_out, slot_ids, gate_vals, w_dense, w_gate, w_up, w_down, ws_gate, ws_up, ws_down):
        flip = functools.partial(jnp.swapaxes, axis1=-1, axis2=-2)
        w1t, w3t, ws1t, ws3t = flip(w_gate), flip(w_up), flip(ws_gate), flip(ws_up)
        weights = [(w_dense[k], w1t[k], w3t[k], w_down[k], ws1t[k], ws3t[k], ws_down[k]) for k in range(2)]
        slot_cols = slot_ids.astype(F32)
        u_one, rows, select, gate, dy_all, act_two = forward_layer(ep, act_in, grad_out, flip(slot_ids), flip(gate_vals), slot_cols[0], gate_vals[0], weights[0])
        two = backward_layer(ep, 1, True, act_two, grad_out, slot_cols[1], weights[1], (dy_all,))
        one = backward_layer(ep, 2, False, act_in, two[0], slot_cols[0], weights[0], (u_one, rows, gate, select))
        sums = []
        for part in (two, one):
            dense = [lax.psum(part[k], ALL_AXES) for k in (1, 5, 6, 7)]
            experts = [lax.psum(part[k], "dp") for k in (2, 3, 4)]
            sums.append((dense, experts))
        dense = [jnp.stack([sums[1][0][k], sums[0][0][k]]) for k in range(4)]
        experts = [jnp.stack([sums[1][1][k], sums[0][1][k]]) for k in range(3)]
        return (one[0], dense[0], flip(experts[0]), flip(experts[1]), experts[2], flip(dense[1]), flip(dense[2]), dense[3])

    return jax.shard_map(body, mesh=mesh, in_specs=(tok_spec, tok_spec, route_spec, route_spec, repl_spec, exp_spec, exp_spec, exp_spec, repl_spec, repl_spec, repl_spec), out_specs=(tok_spec, repl_spec, exp_spec, exp_spec, exp_spec, repl_spec, repl_spec, repl_spec), check_vma=False)
```

time: 769 us -> 649 us (0.84); the launches traced: 759 us -> 648 us
  Pallas kernels: 0 us -> 245 us
  blocking collectives: 94.9 us -> 0 us
  waiting for transfers between devices: 454 us -> 366 us
  local copies, waits for them, and re-layouts: 93.9 us -> 11.7 us
  matrix products: 45.4 us -> 0 us
  starting transfers between devices: 34.9 us -> 0.08 us
  other arithmetic: 20.9 us -> 10.6 us
    pallas_call x0 -> x3, Pallas kernels: none -> 245 us  [the longest x2 140 us: backward_layer(): pl.pallas_call(functools.partial(backward_kernel, (ep, tokens, top, per_e...]
    all_to_all x5 -> x0, waiting for transfers between devices: 141 us -> none  [the longest x2 49.3 us: layer_backward(): lax.all_to_all(grad_rows.reshape(local_exp, ep_size, capacity, width), 'e...]
    all_to_all x2 -> x0, blocking collectives: 94.9 us -> none  [the longest x1 49.8 us: layer_front(): lax.all_to_all(send_buf, 'ep', 0, 1)]
    psum x2, waiting for transfers between devices: 313 us -> 365 us  [the longest x1 292 us: body(): dense = [lax.psum(part[k], ALL_AXES) for k in (1, 5, 6, 7)]]
    dot_general x40 -> x0, matrix products: 45.4 us -> none  [the longest x8 7.41 us: contract_rows(): lax.dot_general(left, right, (((0,), (0,)), ((), ())), preferred_element_...]
    all_to_all x5 -> x0, starting transfers between devices: 34.5 us -> none  [the longest x2 13.5 us: layer_backward(): lax.all_to_all(grad_rows.reshape(local_exp, ep_size, capacity, width), 'e...]
    another operation x15 -> x0, local copies, waits for them, and re-layouts: 32.1 us -> none  [the longest x4 12.6 us: layer_backward(): lax.all_to_all(send_grad, 'ep', 0, 1)]
    gather x7 -> x0, local copies, waits for them, and re-layouts: 30.5 us -> none  [the longest x2 10.9 us: layer_backward(): jnp.take(grad_ext, slot_owner, axis=0)]
  transfers between devices with their start and end apart: 7 -> 2, of which waited for: 7 -> 2; matrix products, arithmetic and copies ran while one was open for 8% -> 1% of each run, Pallas kernels for 0% -> 0%
where the time goes in v1:
time: 649 us; the launch traced here: 648 us
  waiting for transfers between devices  366 us (56%)
  Pallas kernels  245 us (38%)
  between operations  14.1 us (2%)
  local copies, waits for them, and re-layouts  11.7 us (2%)
  other arithmetic  10.6 us (2%)
    psum x1, waiting for transfers between devices, body(): dense = [lax.psum(part[k], ALL_AXES) for k in (1, 5, 6, 7)]  292 us
    pallas_call x2, Pallas kernels, backward_layer(): pl.pallas_call(functools.partial(backward_kernel, (ep, tokens, top, per_e...  140 us
    pallas_call x1, Pallas kernels, forward_layer(): pl.pallas_call(functools.partial(forward_kernel, (ep, tokens, top, per_ex...  106 us
    psum x1, waiting for transfers between devices, body(): experts = [lax.psum(part[k], 'dp') for k in (2, 3, 4)]  73.2 us
  transfers between devices with their start and end apart: 2, of which 2 were waited for; matrix products, arithmetic and copies ran while one was open for 1% of the time, Pallas kernels for 0%

profile of v1, /device:TPU:1, one launch (start us, length us, event | category | flops | bytes accessed | tf_op | source)
XLA Modules:
  0.0 647.6 jit_solution(6695536667018536917)
XLA Ops:
  7.2 0.8 slice.53
  8.0 0.7 copy.21
  8.7 0.8 copy.19
  9.5 0.6 slice_bitcast_fusion.14
  10.2 1.9 slice_bitcast_fusion.12
  12.0 1.1 slice_bitcast_fusion.6
  13.1 1.2 slice_bitcast_fusion.4
  14.5 0.9 slice_bitcast_fusion.8
  15.3 0.8 copy-done.1
  16.1 1.6 slice_bitcast_fusion
  17.7 105.8 %forward_layer.1 = (bf16[96,512]{1,0:T(8,128)(2,1)}, bf16[4,384,512]{2,1,0:T(8,128)(2,1)}, bf16[32,192,128]{2,1,0:T(8,128)(2,1)}, f32[8,192,128]{2,1,0:T(8,128)}...) custom-call(bf16[96,512]{1,0:T(8,128)(2,1)} %refs_0_.1, bf16[96,512]{1,0:T(8,128)(2,1)} %refs_1_.1, ...), custom_call_target="tpu_custom_call" | custom-call | tf_op jit(solution)/shard_map/forward_layer/pallas_call | solution.py:489
  123.5 63.5 %backward_second.1 = (bf16[96,512]{1,0:T(8,128)(2,1)}, bf16[512,512]{1,0:T(8,128)(2,1)}, bf16[4,176,512]{2,1,0:T(8,128)(2,1)}, bf16[4,176,512]{2,1,0:T(8,128)(2,...) custom-call(bf16[96,512]{1,0:T(8,128)(2,1)} %get-tuple-element.30.re, ...), custom_call_target="tpu_custom_call" | custom-call | tf_op jit(solution)/shard_map/backward_second/pallas_call | solution.py:522
  187.0 76.1 %backward_first.1 = (bf16[96,512]{1,0:T(8,128)(2,1)}, bf16[512,512]{1,0:T(8,128)(2,1)}, bf16[4,176,512]{2,1,0:T(8,128)(2,1)}, bf16[4,176,512]{2,1,0:T(8,128)(2,1...) custom-call(bf16[96,512]{1,0:T(8,128)(2,1)} %refs_0_.1, ...), custom_call_target="tpu_custom_call" | custom-call | tf_op jit(solution)/shard_map/backward_first/pallas_call | solution.py:522
  263.2 0.7 all-reduce.7.cloned.1.call-update
  263.9 291.7 %all-reduce.5.cloned.1.call-done = (bf16[1,512,512]{2,1,0:T(8,128)(2,1)}, bf16[1,512,512]{2,1,0:T(8,128)(2,1)}, bf16[1,176,512]{2,1,0:T(8,128)(2,1)}, bf16[1,176...) async-done(((bf16[1,512,512]{2,1,0:T(8,128)(2,1)}, ...) | async-done | bytes 2129936 | tf_op jit(solution)/shard_map/psum | solution.py:550
  555.6 1.9 maximum_bitcast_fusion.2
  557.5 1.8 maximum_bitcast_fusion.3
  559.3 0.8 pad_maximum_fusion.2
  560.0 1.1 pad_maximum_fusion.1
  561.1 73.2 %all-reduce.7.cloned.1.call-done = (bf16[1,4,176,512]{3,2,1,0:T(8,128)(2,1)}, bf16[1,4,176,512]{3,2,1,0:T(8,128)(2,1)}, bf16[1,4,176,512]{3,2,1,0:T(8,128)(2,1)}...) async-done(((bf16[1,4,176,512]{3,2,1,0:T(8,128)(2,1)}, bf16[1,4,176,512]{3,2,1,0:T(8,128)(2,1)}, ...) | async-done | bytes 4325392 | tf_op jit(solution)/shard_map/psum | solution.py:551
  634.3 2.7 maximum_bitcast_fusion
  637.0 1.2 maximum_bitcast_fusion.1
  638.9 1.2 pad_maximum_fusion
  640.1 0.6 copy.37
  (33 shorter events, 0.9 us)
Async XLA Ops:
  7.2 4.9 copy-start.3
  7.2 548.4 %all-reduce.5.cloned.1.call-start = ((), (), s32[]{:S(2)}) async-start(), calls=%async_computation | async-start | bytes 4259840 | tf_op jit(solution)/shard_map/psum | solution.py:550
  10.2 3.0 copy-start
  13.1 1.2 copy-start.10
  13.1 1.3 copy-start.11
  13.1 2.2 copy-start.2
  14.3 1.8 copy-start.1
  263.2 371.2 %all-reduce.7.cloned.1.call-start = ((), (), s32[]{:S(2)}) async-start(), calls=%async_computation.1 | async-start | bytes 8650752 | tf_op jit(solution)/shard_map/psum | solution.py:551
  555.6 3.7 copy-start.12
  555.6 3.7 copy-start.13
  555.6 4.4 copy-start.8
  555.6 4.4 copy-start.9
  634.3 2.7 copy-start.6
  634.3 2.7 copy-start.7
  637.0 1.3 copy-start.4
  637.0 1.8 copy-start.5
  638.9 1.2 copy-start.14
Sparse Core Ops, SparseCore 0:
  263.3 292.2 all-reduce.4
  558.3 75.9 all-reduce.6
